TPU v7x, 32 devices: a whole 2x2x4 slice. The times are simulated.
32 devices in a mesh: group: 2 (over y), batch: 4 (over z), expert: 4 (over x, core).
Axes of the slice: x: 2, y: 2, z: 4, core: 2. Of those that a mesh axis runs over, the one named last changes fastest.
Arguments:
- residual_in: bfloat16 [128, 4096], P(('group', 'batch')), parts along dimension 0, may hold values from -11 to 11
- queries: bfloat16 [128, 16, 128], P(('group', 'batch'), 'expert'), parts along dimension 0, may hold values from -150 to 150
- key_new: bfloat16 [128, 4, 128], P(('group', 'batch'), 'expert'), parts along dimension 0, may hold values from -6 to 6
- value_new: bfloat16 [128, 4, 128], P(('group', 'batch'), 'expert'), parts along dimension 0, may hold values from -6 to 6
- key_cache: bfloat16 [128, 4, 256, 128], P(('group', 'batch'), 'expert'), parts along dimension 0, may hold values from -6 to 6
- value_cache: bfloat16 [128, 4, 256, 128], P(('group', 'batch'), 'expert'), parts along dimension 0, may hold values from -6 to 6
- cache_len: int32 [128], P(('group', 'batch')), parts along dimension 0, may hold values from 1 to 256, 8192 in all
- new_slot: int32 [128], P(('group', 'batch')), parts along dimension 0, may hold values 0 or 1
- out_weight: bfloat16 [2048, 4096], P('expert'), may hold values from -0.125 to 0.125
- norm_gain: float32 [4096], replicated, may hold values from 0.5 to 1.5
- router: bfloat16 [4096, 4], replicated, may hold values from -0.09375 to 0.09375
- chosen: int32 [128, 2], P(('group', 'batch')), parts along dimension 0, may hold values from 0 to 3, all different within a row; in each aligned block of 16 rows (0 to 15, 16 to 31, ...) at most 12 rows name the same one
- w_gate: bfloat16 [4, 4096, 8192], P('expert', None, 'batch'), may hold values from -0.09375 to 0.09375
- w_up: bfloat16 [4, 4096, 8192], P('expert', None, 'batch'), may hold values from -0.09375 to 0.09375
- w_down: bfloat16 [4, 8192, 4096], P('expert', 'batch'), may hold values from -0.0625 to 0.0625
Outputs:
- layer_out: bfloat16 [128, 4096], P(('group', 'batch', 'expert')), parts along dimension 0
There are 2 independent parts, one for each index of `group`. A program takes and returns all parts, laid end to end along the dimension named above; an argument that names none is the same for every part. Nothing has to cross between parts.
Inputs may be any that keep to these rules, and one draw needn't show every extreme that they name: `chosen`: each row names 2 different experts. Among the rows of one device no expert is named by more than 12 rows, and in every draw some expert is named by exactly 12 rows of some device. `cache_len`: the lengths of a part sum to 8192, and the largest is exactly 256.
All inputs are finite; a program needn't handle non-finite values. No bound on the sum of `cache_len` or of `new_slot` on one device may be relied on, other than what follows from the above.
Results may differ from a plain program's by a relative error of at most 0.017.
Values may be sent and summed in bfloat16 or wider, within the bound.
No kernel may reach another device: no remote copies, remote signals or barrier semaphores. Data moves between devices by JAX's collectives and lax.ppermute only.
A program may use at most 128 MiB of HBM per device.

v0:
```python
import jax
import jax.numpy as jnp
from jax import lax
from jax.sharding import PartitionSpec as P

CAP = 12
epsilon = 1e-05


def attend(queries, key_new, value_new, key_cache, value_cache, cache_len, new_slot):
    slot_count, kv_count, length, head_width = key_cache.shape
    group_size = queries.shape[1] // kv_count
    grouped = queries.reshape(slot_count, kv_count, group_size, head_width)
    scaling = float(head_width) ** (-0.5)
    scores = (
        jnp.einsum("skgd,sktd->skgt", grouped, key_cache, preferred_element_type=jnp.float32)
        * scaling
    )
    own_score = (
        jnp.einsum("skgd,skd->skg", grouped, key_new, preferred_element_type=jnp.float32) * scaling
    )
    places = lax.broadcasted_iota(jnp.int32, (slot_count, length), 1)
    usable = (places < cache_len[:, None]) & (new_slot[:, None] == 0)
    usable = usable[:, None, None, :]
    scores = jnp.where(usable, scores, jnp.float32(-1e30))
    highest = jnp.maximum(jnp.max(scores, axis=3), own_score)
    weights = jnp.where(usable, jnp.exp(scores - highest[..., None]), jnp.float32(0.0))
    own_weight = jnp.exp(own_score - highest)
    denominator = jnp.sum(weights, axis=3) + own_weight
    probabilities = (weights / denominator[..., None]).astype(jnp.bfloat16)
    own_prob = (own_weight / denominator).astype(jnp.bfloat16)
    attended = jnp.einsum(
        "skgt,sktd->skgd", probabilities, value_cache, preferred_element_type=jnp.float32
    )
    attended = (
        attended
        + own_prob.astype(jnp.float32)[..., None] * value_new.astype(jnp.float32)[:, :, None, :]
    )
    return attended.reshape(slot_count, kv_count * group_size * head_width).astype(jnp.bfloat16)


def mixing(logits, chosen, expert_count):
    labels = lax.broadcasted_iota(jnp.int32, (1, 1, expert_count), 2)
    picking = (chosen[:, :, None] == labels).astype(jnp.float32)
    chosen_logits = jnp.sum(picking * logits[:, None, :], axis=2)
    leading = jax.nn.sigmoid(chosen_logits[:, 0] - chosen_logits[:, 1])
    fractions = jnp.stack([leading, 1.0 - leading], axis=1)
    return jnp.sum(picking * fractions[:, :, None], axis=1)


def placement_table(chosen, targets, capacity):
    routed = jnp.sum((chosen[None, :, :] == targets[:, None, None]).astype(jnp.int32), axis=2)
    position = jnp.cumsum(routed, axis=1) - routed
    row_labels = lax.broadcasted_iota(jnp.int32, (1, capacity, 1), 1)
    return ((position[:, None, :] == row_labels) & (routed[:, None, :] == 1)).astype(jnp.float32)


def body(
    residual_in,
    queries,
    key_new,
    value_new,
    key_cache,
    value_cache,
    cache_len,
    new_slot,
    out_weight,
    norm_gain,
    router,
    chosen,
    w_gate,
    w_up,
    w_down,
):
    my_expert = lax.axis_index("expert")
    attended = attend(queries, key_new, value_new, key_cache, value_cache, cache_len, new_slot)
    partial_value = jnp.dot(attended, out_weight, preferred_element_type=jnp.float32)
    summed = lax.psum(partial_value, "expert")
    stream = (residual_in.astype(jnp.float32) + summed).astype(jnp.bfloat16)
    values = stream.astype(jnp.float32)
    scaling = lax.rsqrt(jnp.mean(values * values, axis=1, keepdims=True) + epsilon)
    normed = (values * scaling * norm_gain).astype(jnp.bfloat16)
    logits = jnp.dot(normed, router, preferred_element_type=jnp.float32)
    placing = placement_table(chosen, jnp.reshape(my_expert, (1,)), CAP)[0]
    sent_rows = jnp.dot(
        placing.astype(jnp.bfloat16), normed, preferred_element_type=jnp.float32
    ).astype(jnp.bfloat16)
    carried = values * (my_expert == 0).astype(jnp.float32)
    coef = mixing(logits, chosen, router.shape[1])
    expert_labels = lax.broadcasted_iota(jnp.int32, (1, router.shape[1]), 1)
    my_coef = jnp.sum(coef * (expert_labels == my_expert).astype(jnp.float32), axis=1)
    row_weight = jnp.dot(placing, my_coef, precision=lax.Precision.HIGHEST)
    block_rows = lax.all_gather(sent_rows, "batch", axis=0, tiled=True)
    gate_part = jnp.dot(block_rows, w_gate[0], preferred_element_type=jnp.float32)
    up_part = jnp.dot(block_rows, w_up[0], preferred_element_type=jnp.float32)
    hidden = (jax.nn.silu(gate_part) * up_part).astype(jnp.bfloat16)
    block_rows = hidden
    outputs = lax.psum_scatter(
        jnp.dot(block_rows, w_down[0], preferred_element_type=jnp.float32).astype(jnp.bfloat16),
        "batch",
        scatter_dimension=0,
        tiled=True,
    ).astype(jnp.float32)
    weighted = row_weight[:, None] * outputs
    contribution = jnp.dot(placing.T, weighted, precision=lax.Precision.HIGHEST) + carried
    layer_out = lax.psum_scatter(
        contribution.astype(jnp.bfloat16), "expert", scatter_dimension=0, tiled=True
    )
    return layer_out


def solution(mesh):
    in_specs = (
        P(("group", "batch"), None),
        P(("group", "batch"), "expert", None),
        P(("group", "batch"), "expert", None),
        P(("group", "batch"), "expert", None),
        P(("group", "batch"), "expert", None, None),
        P(("group", "batch"), "expert", None, None),
        P(("group", "batch")),
        P(("group", "batch")),
        P("expert", None),
        P(),
        P(),
        P(("group", "batch"), None),
        P("expert", None, "batch"),
        P("expert", None, "batch"),
        P("expert", "batch", None),
    )
    out_specs = P(("group", "batch", "expert"), None)
    return jax.shard_map(body, mesh=mesh, in_specs=in_specs, out_specs=out_specs, check_vma=False)
```

profile of v0, /device:TPU:0, one launch (start us, length us, event | category | flops | bytes accessed | tf_op | source)
XLA Modules:
  0.0 154.4 jit_solution(7242869067965577408)
XLA Ops:
  6.5 0.0 copy-start
  6.5 0.0 all-reduce.6.cloned.1.call-start
  6.5 0.7 broadcast_compare_fusion
  7.3 0.7 fusion.48
  8.0 0.9 fusion.52
  8.9 0.0 copy-done
  8.9 1.2 fusion.67
  10.1 0.2 fusion.37
  10.3 0.7 bitcast_convert_fusion
  11.0 1.5 fusion.19
  12.5 3.6 %fusion.45 = f32[16,4096]{1,0:T(8,128)} fusion(bf16[512,4096]{1,0:T(8,128)(2,1)} %param.23, bf16[2,8,4,128]{3,2,1,0:T(4,128)(2,1)S(1)} %bitcast.56), kind=kOutput, calls=%fused_computation.45 | convolution fusion | flops 67108864 | bytes 4472832 | tf_op jit(solution)/shard_map/dot_general | solution.py:77
  16.1 0.0 all-reduce.6.cloned.1.call-update
  16.1 0.0 all-reduce.8.cloned.1.call-start
  16.1 0.7 fusion.63
  16.8 0.1 copy.26
  17.0 0.1 reduce.6
  17.1 1.2 dynamic-slice.6
  19.0 32.2 %all-reduce.6.cloned.1.call-done = f32[16,4096]{1,0:T(8,128)} async-done(((f32[16,4096]{1,0:T(8,128)}), f32[16,4096]{1,0:T(8,128)}) %all-reduce.6.cloned.1.call-update) | async-done | bytes 262160 | tf_op jit(solution)/shard_map/psum | solution.py:78
  51.2 1.1 fusion.29
  52.4 1.0 fusion.11
  53.3 15.2 %all-gather = bf16[4,12,4096]{2,1,0:T(8,128)(2,1)S(1)} all-gather(bf16[1,12,4096]{2,1,0:T(8,128)(2,1)S(1)} %fusion.11), channel_id=1, replica_groups=mesh['group'=2,'batch'=4,'expert'=4] {'batch'}, dimensions={0}, use_global_device_ids=true | all-gather | bytes 491520 | tf_op jit(solution)/shard_map/all_gather | solution.py:93
  68.5 0.1 reshape.221
  68.6 8.8 %fusion.5 = f32[48,2048]{1,0:T(8,128)S(1)} fusion(bf16[48,4096]{1,0:T(8,128)(2,1)S(1)} %reshape.221, bf16[1,4096,2048]{2,1,0:T(8,128)(2,1)} %param.27), kind=kOutput, calls=%fused_computation.4 | convolution fusion | flops 805306368 | bytes 17563648 | tf_op jit(solution)/shard_map/dot_general | solution.py:94
  77.4 0.0 copy-start.1
  77.4 0.0 copy-start.3
  77.4 0.0 copy-start.2
  77.4 0.0 copy-start.4
  77.5 13.7 %fusion.7 = bf16[48,4096]{1,0:T(8,128)(2,1)S(1)} fusion(bf16[1,2048,4096]{2,1,0:T(8,128)(2,1)} %param.29, bf16[48,4096]{1,0:T(8,128)(2,1)S(1)} %reshape.221, bf16[1,4096,2048]{2,1,0:T(8,128)(2,1)} %param.28, f32[48,2048]{1,0:T(8,128)S(1)} %fusion.5), kind=kOutput, calls=%fused_computation.6 | convolution fusion | flops 1611399168 | bytes 34734080 | tf_op jit(solution)/shard_map/dot_general | solution.py:99
  91.1 16.0 %fusion = bf16[16,4096]{1,0:T(8,128)(2,1)S(1)} fusion(bf16[48,4096]{1,0:T(8,128)(2,1)S(1)} %fusion.7), kind=kCustom, calls=%all-reduce-scatter | all-reduce-scatter fusion | flops 262145 | bytes 524800
  107.2 2.8 %collective-permute-start = (bf16[12,4096]{1,0:T(8,128)(2,1)S(1)}, bf16[12,4096]{1,0:T(8,128)(2,1)S(1)}, u32[]{:S(2)}, u32[]{:S(2)}) collective-permute-start(bf16[12,4096]{1,0:T(8,128)(2,1)S(1)} %slice.8), channel_id=1, source_target_pairs={{0,4},{4,8},{8,12},{1,5},{5,9},{9,13},{2,6},{6,10},{10,14},{3,7},{... | collective-permute-start | bytes 294920
  110.0 0.0 copy-done.1
  110.1 0.0 copy-done.3
  110.1 0.2 fusion.43
  110.3 0.0 copy-done.2
  110.4 0.1 multiply_reduce_fusion
  110.5 0.1 convolution_bitcast_fusion
  110.6 2.0 %collective-permute-done = bf16[12,4096]{1,0:T(8,128)(2,1)S(1)} collective-permute-done((bf16[12,4096]{1,0:T(8,128)(2,1)S(1)}, bf16[12,4096]{1,0:T(8,128)(2,1)S(1)}, u32[]{:S(2)}, u32[]{:S(2)}) %collective-permute-start) | collective-permute-done | bytes 98336
  112.5 0.3 concatenate
  112.9 1.0 fusion.10
  113.9 0.0 all-reduce.8.cloned.1.call-update
  113.9 0.0 copy-done.4
  113.9 0.6 dynamic-slice.2
  115.1 31.0 %all-reduce.8.cloned.1.call-done = bf16[16,4096]{1,0:T(8,128)(2,1)} async-done(((bf16[16,4096]{1,0:T(8,128)(2,1)}), bf16[16,4096]{1,0:T(8,128)(2,1)}) %all-reduce.8.cloned.1.call-update) | async-done | bytes 131088
  146.1 1.5 constant_dynamic-slice_fusion
  (12 shorter events, 0.2 us)
Async XLA Ops:
  6.5 2.3 %copy-start = (bf16[16,1,256,128]{3,2,1,0:T(8,128)(2,1)S(1)}, bf16[16,1,256,128]{3,2,1,0:T(8,128)(2,1)}, u32[]{:S(2)}) copy-start(bf16[16,1,256,128]{3,2,1,0:T(8,128)(2,1)} %param.19) | copy-start | bytes 3145732
  6.5 44.7 %all-reduce.6.cloned.1.call-start = ((), (), s32[]{:S(2)}) async-start(), calls=%async_computation | async-start | bytes 524288 | tf_op jit(solution)/shard_map/psum | solution.py:78
  16.1 130.0 %all-reduce.8.cloned.1.call-start = ((), (), s32[]{:S(2)}) async-start(), calls=%async_computation.1 | async-start | bytes 262144
  77.4 32.6 %copy-start.1 = (f32[4096]{0:T(1024)S(1)}, f32[4096]{0:T(1024)}, u32[]{:S(2)}) copy-start(f32[4096]{0:T(1024)} %param.24) | copy-start | bytes 49156
  77.4 32.6 %copy-start.3 = (bf16[4096,4]{0,1:T(4,128)(2,1)S(1)}, bf16[4096,4]{0,1:T(4,128)(2,1)}, u32[]{:S(2)}) copy-start(bf16[4096,4]{0,1:T(4,128)(2,1)} %param.25) | copy-start | bytes 98308
  77.4 32.9 %copy-start.2 = (s32[16,2]{0,1:T(2,128)S(1)}, s32[16,2]{0,1:T(2,128)}, u32[]{:S(2)}) copy-start(s32[16,2]{0,1:T(2,128)} %param.26) | copy-start | bytes 388
  77.4 36.4 %copy-start.4 = (u32[32]{0:T(128)S(1)}, u32[32]{0:T(128)}, u32[]{:S(2)}) copy-start(u32[32]{0:T(128)} %constant.45) | copy-start | bytes 388
  107.2 5.4 %collective-permute-start = (bf16[12,4096]{1,0:T(8,128)(2,1)S(1)}, bf16[12,4096]{1,0:T(8,128)(2,1)S(1)}, u32[]{:S(2)}, u32[]{:S(2)}) collective-permute-start(bf16[12,4096]{1,0:T(8,128)(2,1)S(1)} %slice.8), channel_id=1, source_target_pairs={{0,4},{4,8},{8,12},{1,5},{5,9},{9,13},{2,6},{6,10},{10,14},{3,7},{... | collective-permute-start | bytes 294920
Sparse Core Ops, SparseCore 0:
  16.2 34.9 all-reduce.5
  114.0 32.0 all-reduce.7
where the time goes:
time: 155 us; the launch traced here: 154 us
  waiting for transfers between devices  65.2 us (42%)
  matrix products  31.9 us (21%)
  blocking collectives  31.2 us (20%)
  between operations  14.9 us (10%)
  other arithmetic  4.53 us (3%)
  local copies, waits for them, and re-layouts  3.85 us (2%)
  starting transfers between devices  2.89 us (2%)
    unnamed x4, waiting for transfers between devices  33 us
    psum x1, waiting for transfers between devices, body(): summed = lax.psum(partial_value, 'expert')  32.2 us
    unnamed x1, blocking collectives  16 us
    all_gather x1, blocking collectives, body(): block_rows = lax.all_gather(sent_rows, 'batch', axis=0, tiled=True)  15.2 us
    dot_general x1, matrix products, body(): jnp.dot(block_rows, w_down[0], preferred_element_type=jnp.float32)  13.7 us
    dot_general x1, matrix products, body(): jnp.dot(block_rows, w_gate[0], preferred_element_type=jnp.float32)  8.79 us
    unnamed x16, local copies, waits for them, and re-layouts  3.76 us
    dot_general x1, matrix products, body(): jnp.dot(attended, out_weight, preferred_element_type=jnp.float32)  3.56 us
  transfers between devices with their start and end apart: 3, of which 3 were waited for; matrix products, arithmetic and copies ran while one was open for 2% of the time, Pallas kernels for 0%

commit v1 on v0

--- a/solution.py
+++ b/solution.py
@@ -75,7 +75,9 @@
     my_expert = lax.axis_index("expert")
     attended = attend(queries, key_new, value_new, key_cache, value_cache, cache_len, new_slot)
     partial_value = jnp.dot(attended, out_weight, preferred_element_type=jnp.float32)
-    summed = lax.psum(partial_value, "expert")
+    summed = partial_value
+    for hop in (1, 2):
+        summed = summed + lax.ppermute(summed, "expert", [(dev, dev ^ hop) for dev in range(4)])
     stream = (residual_in.astype(jnp.float32) + summed).astype(jnp.bfloat16)
     values = stream.astype(jnp.float32)
     scaling = lax.rsqrt(jnp.mean(values * values, axis=1, keepdims=True) + epsilon)

time: 155 us -> 134 us (0.86)
  waiting for transfers between devices: 65.2 us -> 38.6 us
  starting transfers between devices: 2.89 us -> 5.87 us
  blocking collectives: 31.2 us -> 32.8 us
    psum x1 -> x0, waiting for transfers between devices: 32.2 us -> none  [body(): summed = lax.psum(partial_value, 'expert')]
    ppermute x0 -> x2, waiting for transfers between devices: none -> 4.91 us  [body(): lax.ppermute(summed, 'expert', [(dev, dev ^ hop) for dev in range(4)])]
    ppermute x0 -> x2, starting transfers between devices: none -> 3.41 us  [body(): lax.ppermute(summed, 'expert', [(dev, dev ^ hop) for dev in range(4)])]
    unnamed x4 -> x3, waiting for transfers between devices: 33 us -> 33.7 us
    unnamed x16 -> x10, local copies, waits for them, and re-layouts: 3.76 us -> 3.74 us
  transfers between devices with their start and end apart: 3 -> 4, of which waited for: 3 -> 4; matrix products, arithmetic and copies ran while one was open for 2% -> 2% of each run, Pallas kernels for 0% -> 0%
where the time goes in v1:
time: 134 us
  waiting for transfers between devices  38.6 us (29%)
  blocking collectives  32.8 us (24%)
  matrix products  31.9 us (24%)
  between operations  14.8 us (11%)
  starting transfers between devices  5.87 us (4%)
  other arithmetic  5.86 us (4%)
  local copies, waits for them, and re-layouts  3.83 us (3%)
    unnamed x3, waiting for transfers between devices  33.7 us
    unnamed x1, blocking collectives  17.1 us
    all_gather x1, blocking collectives, body(): block_rows = lax.all_gather(sent_rows, 'batch', axis=0, tiled=True)  15.7 us
    dot_general x1, matrix products, body(): jnp.dot(block_rows, w_down[0], preferred_element_type=jnp.float32)  13.7 us
    dot_general x1, matrix products, body(): jnp.dot(block_rows, w_gate[0], preferred_element_type=jnp.float32)  8.79 us
    ppermute x2, waiting for transfers between devices, body(): lax.ppermute(summed, 'expert', [(dev, dev ^ hop) for dev in range(4)])  4.91 us
    unnamed x10, local copies, waits for them, and re-layouts  3.74 us
    ppermute x2, starting transfers between devices, body(): lax.ppermute(summed, 'expert', [(dev, dev ^ hop) for dev in range(4)])  3.41 us
  transfers between devices with their start and end apart: 4, of which 4 were waited for; matrix products, arithmetic and copies ran while one was open for 2% of the time, Pallas kernels for 0%

profile of v1, /device:TPU:0, one launch (start us, length us, event | category | flops | bytes accessed | tf_op | source)
XLA Modules:
  0.0 133.6 jit_solution(3723533601127072040)
XLA Ops:
  6.5 0.0 copy-start
  6.5 0.0 all-reduce.5.cloned.1.call-start
  6.5 0.7 broadcast_compare_fusion
  7.3 0.7 fusion.48
  8.0 0.9 fusion.52
  8.9 0.0 copy-done
  8.9 1.2 fusion.67
  10.1 0.2 fusion.37
  10.3 0.7 bitcast_convert_fusion
  11.0 1.5 %fusion.19 = bf16[16,4,128]{2,1,0:T(4,128)(2,1)S(1)} fusion(bf16[16,1,256,128]{3,2,1,0:T(8,128)(2,1)} %param.20, f32[16,4,256]{2,1,0:T(4,128)S(1)} %get-tuple-element.12, f32[16,4]{1,0:T(8,128)S(1)} %get-tuple-element.10, f32[16,4]{1,0:T(8,128)S(1)} %multiply_maximum_fusion, pred[16,256]{1,0:T(8,128)(4,1)S(1)} %fusion.48, ...), kind=kOutput, calls=%fused_computation.16 | convolution fusion | flops 4284416 | bytes 1143552 | tf_op jit(solution)/shard_map/skgt,sktd->skgd/dot_general | solution.py:32
  12.5 2.9 %fusion.45 = f32[16,4096]{1,0:T(8,128)S(1)} fusion(bf16[512,4096]{1,0:T(8,128)(2,1)} %param.23, bf16[2,8,4,128]{3,2,1,0:T(4,128)(2,1)S(1)} %bitcast.56), kind=kOutput, calls=%fused_computation.45 | convolution fusion | flops 67108864 | bytes 4472832 | tf_op jit(solution)/shard_map/dot_general | solution.py:77
  15.4 0.5 collective-permute-start
  15.9 0.7 fusion.63
  16.6 0.5 collective-permute-done
  17.1 2.9 %collective-permute-start.1 = (f32[16,4096]{1,0:T(8,128)S(1)}, f32[16,4096]{1,0:T(8,128)S(1)}, u32[]{:S(2)}, u32[]{:S(2)}) collective-permute-start(f32[16,4096]{1,0:T(8,128)S(1)} %add.43), channel_id=1, source_target_pairs={{0,2},{1,3},{2,0},{3,1},{4,6},{5,7},{6,4},{7,5},{8,10},{9,11},{10,... | collective-permute-start | bytes 786440 | tf_op jit(solution)/shard_map/ppermute | solution.py:80
  20.0 0.1 copy.26
  20.1 0.1 reduce.6
  20.2 1.2 dynamic-slice.6
  22.1 4.4 %collective-permute-done.1 = f32[16,4096]{1,0:T(8,128)S(1)} collective-permute-done((f32[16,4096]{1,0:T(8,128)S(1)}, f32[16,4096]{1,0:T(8,128)S(1)}, u32[]{:S(2)}, u32[]{:S(2)}) %collective-permute-start.1) | collective-permute-done | bytes 262176 | tf_op jit(solution)/shard_map/ppermute | solution.py:80
  26.6 1.1 fusion.29
  27.6 1.0 fusion.43
  28.6 0.7 select_reduce_fusion.1
  29.4 0.7 select_reduce_fusion
  30.1 0.9 fusion.11
  31.0 15.7 %all-gather = bf16[4,12,4096]{2,1,0:T(8,128)(2,1)S(1)} all-gather(bf16[1,12,4096]{2,1,0:T(8,128)(2,1)S(1)} %fusion.11), channel_id=1, replica_groups=mesh['group'=2,'batch'=4,'expert'=4] {'batch'}, dimensions={0}, use_global_device_ids=true | all-gather | bytes 491520 | tf_op jit(solution)/shard_map/all_gather | solution.py:95
  46.7 0.1 reshape.221
  46.8 8.8 %fusion.5 = f32[48,2048]{1,0:T(8,128)S(1)} fusion(bf16[48,4096]{1,0:T(8,128)(2,1)S(1)} %reshape.221, bf16[1,4096,2048]{2,1,0:T(8,128)(2,1)} %param.27), kind=kOutput, calls=%fused_computation.4 | convolution fusion | flops 805306368 | bytes 17563648 | tf_op jit(solution)/shard_map/dot_general | solution.py:96
  55.6 0.0 copy-start.1
  55.6 13.7 %fusion.7 = bf16[48,4096]{1,0:T(8,128)(2,1)S(1)} fusion(bf16[1,2048,4096]{2,1,0:T(8,128)(2,1)} %param.29, bf16[48,4096]{1,0:T(8,128)(2,1)S(1)} %reshape.221, bf16[1,4096,2048]{2,1,0:T(8,128)(2,1)} %param.28, f32[48,2048]{1,0:T(8,128)S(1)} %fusion.5), kind=kOutput, calls=%fused_computation.6 | convolution fusion | flops 1611399168 | bytes 34734080 | tf_op jit(solution)/shard_map/dot_general | solution.py:101
  69.3 17.1 %fusion = bf16[16,4096]{1,0:T(8,128)(2,1)S(1)} fusion(bf16[48,4096]{1,0:T(8,128)(2,1)S(1)} %fusion.7), kind=kCustom, calls=%all-reduce-scatter | all-reduce-scatter fusion | flops 262145 | bytes 524800
  86.4 2.5 %collective-permute-start.2 = (bf16[12,4096]{1,0:T(8,128)(2,1)S(1)}, bf16[12,4096]{1,0:T(8,128)(2,1)S(1)}, u32[]{:S(2)}, u32[]{:S(2)}) collective-permute-start(bf16[12,4096]{1,0:T(8,128)(2,1)S(1)} %slice.8), channel_id=1, source_target_pairs={{0,4},{4,8},{8,12},{1,5},{5,9},{9,13},{2,6},{6,10},{10,14},{3,7},{... | collective-permute-start | bytes 294920
  88.9 0.1 multiply_reduce_fusion
  89.0 0.1 convolution_bitcast_fusion
  89.1 2.3 %collective-permute-done.2 = bf16[12,4096]{1,0:T(8,128)(2,1)S(1)} collective-permute-done((bf16[12,4096]{1,0:T(8,128)(2,1)S(1)}, bf16[12,4096]{1,0:T(8,128)(2,1)S(1)}, u32[]{:S(2)}, u32[]{:S(2)}) %collective-permute-start.2) | collective-permute-done | bytes 98336
  91.4 0.3 concatenate
  91.7 1.0 fusion.10
  92.7 0.0 all-reduce.5.cloned.1.call-update
  92.7 0.0 copy-done.1
  92.7 0.6 dynamic-slice.2
  94.0 31.3 %all-reduce.5.cloned.1.call-done = bf16[16,4096]{1,0:T(8,128)(2,1)} async-done(((bf16[16,4096]{1,0:T(8,128)(2,1)}), bf16[16,4096]{1,0:T(8,128)(2,1)}) %all-reduce.5.cloned.1.call-update) | async-done | bytes 131088
  125.3 1.5 %constant_dynamic-slice_fusion = bf16[4,4096]{1,0:T(4,128)(2,1)} fusion(bf16[16,4096]{1,0:T(8,128)(2,1)} %all-reduce.5.cloned.1.call-done, u32[]{:T(128)S(6)} %multiply.9), kind=kLoop, calls=%fused_computation.76 | loop fusion | bytes 65540
  (11 shorter events, 0.2 us)
Async XLA Ops:
  6.5 2.3 %copy-start = (bf16[16,1,256,128]{3,2,1,0:T(8,128)(2,1)S(1)}, bf16[16,1,256,128]{3,2,1,0:T(8,128)(2,1)}, u32[]{:S(2)}) copy-start(bf16[16,1,256,128]{3,2,1,0:T(8,128)(2,1)} %param.19) | copy-start | bytes 3145732
  6.5 118.8 %all-reduce.5.cloned.1.call-start = ((), (), s32[]{:S(2)}) async-start(), calls=%async_computation | async-start | bytes 262144
  15.4 1.7 %collective-permute-start = (f32[16,4096]{1,0:T(8,128)S(1)}, f32[16,4096]{1,0:T(8,128)S(1)}, u32[]{:S(2)}, u32[]{:S(2)}) collective-permute-start(f32[16,4096]{1,0:T(8,128)S(1)} %fusion.45), channel_id=1, source_target_pairs={{0,1},{1,0},{2,3},{3,2},{4,5},{5,4},{6,7},{7,6},{8,9},{9,8},{10,11... | collective-permute-start | bytes 786440 | tf_op jit(solution)/shard_map/ppermute | solution.py:80
  17.1 9.5 %collective-permute-start.1 = (f32[16,4096]{1,0:T(8,128)S(1)}, f32[16,4096]{1,0:T(8,128)S(1)}, u32[]{:S(2)}, u32[]{:S(2)}) collective-permute-start(f32[16,4096]{1,0:T(8,128)S(1)} %add.43), channel_id=1, source_target_pairs={{0,2},{1,3},{2,0},{3,1},{4,6},{5,7},{6,4},{7,5},{8,10},{9,11},{10,... | collective-permute-start | bytes 786440 | tf_op jit(solution)/shard_map/ppermute | solution.py:80
  55.6 37.1 %copy-start.1 = (u32[32]{0:T(128)S(1)}, u32[32]{0:T(128)}, u32[]{:S(2)}) copy-start(u32[32]{0:T(128)} %constant.45) | copy-start | bytes 388
  86.4 5.0 %collective-permute-start.2 = (bf16[12,4096]{1,0:T(8,128)(2,1)S(1)}, bf16[12,4096]{1,0:T(8,128)(2,1)S(1)}, u32[]{:S(2)}, u32[]{:S(2)}) collective-permute-start(bf16[12,4096]{1,0:T(8,128)(2,1)S(1)} %slice.8), channel_id=1, source_target_pairs={{0,4},{4,8},{8,12},{1,5},{5,9},{9,13},{2,6},{6,10},{10,14},{3,7},{... | collective-permute-start | bytes 294920
Sparse Core Ops, SparseCore 0:
  92.8 32.4 all-reduce.4
